TPU v7x, 512 devices: a whole 4x4x16 slice. The times are simulated.
512 devices in a mesh: dp: 64 (over z, x), head: 8 (over y, core).
Axes of the slice: x: 4, y: 4, z: 16, core: 2. Of those that a mesh axis runs over, the one named last changes fastest.
Arguments:
- queries: bfloat16 [16384, 8192], P('dp', 'head'), may hold values from -6 to 6
- keys: bfloat16 [16384, 1024], P('dp', 'head'), may hold values from -6 to 6
- values: bfloat16 [16384, 1024], P('dp', 'head'), may hold values from -6 to 6
- output_grad: bfloat16 [16384, 4096], P('dp', 'head'), may hold values from -6 to 6
- out_weight: bfloat16 [8192, 4096], P(('head', 'dp')), may hold values from -0.0625 to 0.0625
- lengths: int32 [64], replicated, may hold values from 1 to 512, 16384 in all
Outputs:
- layer_out: bfloat16 [16384, 4096], P('dp', 'head')
- query_grad: bfloat16 [16384, 8192], P('dp', 'head')
- key_grad: bfloat16 [16384, 1024], P('dp', 'head')
- value_grad: bfloat16 [16384, 1024], P('dp', 'head')
Inputs may be any that keep to these rules, and one draw needn't show every extreme that they name: Each of the 64 lengths is at least 1 and at most 512, they sum to 16384, and one equals 512.
All inputs are finite; a program needn't handle non-finite values.
Results may differ from a plain program's by a relative error of at most 0.028.
Values may be sent and summed in bfloat16 or wider, within the bound.
No kernel may reach another device: no remote copies, remote signals or barrier semaphores. Data moves between devices by JAX's collectives and lax.ppermute only.
A program may use at most 128 MiB of HBM per device.

v0:
```python
import math
import jax
import jax.numpy as jnp
from jax import lax
from jax.sharding import Mesh
from jax.sharding import PartitionSpec as P

HD = 128
SPAN = 2
DP = ("dp_0", "dp_1")
HEAD_DP = ("head", "dp_0", "dp_1")
masked_score = -1e30


def gather_axes(x, axes, dim):
    filled = x
    for number in range(len(axes) - 1, -1, -1):
        filled = lax.all_gather(filled, axes[number], axis=dim, tiled=True)
    return filled


def in_order(pieces, dim):
    pieces = jnp.moveaxis(pieces, 0, dim)
    shape = pieces.shape
    return pieces.reshape(*shape[:dim], shape[dim] * shape[dim + 1], *shape[dim + 2 :])


def from_everyone(x, axis):
    size = lax.axis_size(axis)
    return lax.all_to_all(jnp.broadcast_to(x[None], (size, *x.shape)), axis, 0, 0, tiled=True)


def gather_directly(x, axis, dim):
    return in_order(from_everyone(x, axis), dim)


def passed_along(block, axis, distance):
    devices = range(lax.axis_size(axis))
    route = [(i - distance, i) for i in devices if i - distance in devices]
    return lax.ppermute(block, axis, route)


def in_blocks(x, dim, size):
    before, after = (x.shape[:dim], x.shape[dim + 1 :])
    return jnp.moveaxis(x.reshape(*before, size, -1, *after), dim, 0)


def sent_and_summed(x, axis, dim):
    pieces = in_blocks(x, dim, lax.axis_size(axis))
    arrived = lax.all_to_all(pieces, axis, split_axis=0, concat_axis=0, tiled=True)
    return arrived.astype(jnp.float32).sum(axis=0)


def doc_start(lengths, positions):
    doc_ends = jnp.cumsum(lengths)
    closed = doc_ends[None, :] <= positions[:, None]
    return jnp.sum(jnp.where(closed, lengths[None, :], 0), axis=1)


def attend(queries, key_rows, value_rows, d_attended, visible, head_dim):
    row_count = queries.shape[0]
    kv_heads = key_rows.shape[1] // head_dim
    group_ratio = queries.shape[1] // key_rows.shape[1]
    scaling = 1.0 / math.sqrt(head_dim)
    grouped = queries.reshape(row_count, kv_heads, group_ratio, head_dim)
    keyed = key_rows.reshape(-1, kv_heads, head_dim)
    valued = value_rows.reshape(-1, kv_heads, head_dim)
    upstream = d_attended.reshape(row_count, kv_heads, group_ratio, head_dim)
    scores = (
        jnp.einsum("tgrd,ngd->grtn", grouped, keyed, preferred_element_type=jnp.float32) * scaling
    )
    scores = jnp.where(visible[None, None], scores, masked_score)
    maximum = jnp.max(scores, axis=-1, keepdims=True)
    weights = jnp.exp(scores - maximum)
    shares = weights / jnp.sum(weights, axis=-1, keepdims=True)
    shares_low = shares.astype(jnp.bfloat16)
    attended = jnp.einsum(
        "grtn,ngd->tgrd", shares_low, valued, preferred_element_type=jnp.float32
    ).astype(jnp.bfloat16)
    row_dots = jnp.sum(upstream.astype(jnp.float32) * attended.astype(jnp.float32), axis=-1)
    d_shares = jnp.einsum("tgrd,ngd->grtn", upstream, valued, preferred_element_type=jnp.float32)
    dscore = (shares * (d_shares - jnp.transpose(row_dots, (1, 2, 0))[..., None]) * scaling).astype(
        jnp.bfloat16
    )
    query_grad = jnp.einsum(
        "grtn,ngd->tgrd", dscore, keyed, preferred_element_type=jnp.float32
    ).astype(jnp.bfloat16)
    key_part = jnp.einsum("grtn,tgrd->ngd", dscore, grouped, preferred_element_type=jnp.float32)
    value_part = jnp.einsum(
        "grtn,tgrd->ngd", shares_low, upstream, preferred_element_type=jnp.float32
    )
    return (
        attended.reshape(row_count, -1),
        query_grad.reshape(row_count, -1),
        key_part.reshape(-1, kv_heads * head_dim),
        value_part.reshape(-1, kv_heads * head_dim),
    )


def on_device(queries, keys, values, output_grad, out_weight, lengths):
    block_rows = queries.shape[0]
    device = lax.axis_index(DP)
    group_weight = lax.all_gather(out_weight, DP, axis=0, tiled=True)
    upstream_all = gather_directly(output_grad, "head", 1)
    d_attended = jnp.einsum(
        "tc,rc->tr", upstream_all, group_weight, preferred_element_type=jnp.float32
    ).astype(jnp.bfloat16)
    earlier = [passed_along((keys, values), DP, offset) for offset in range(1, SPAN + 1)]
    key_rows = jnp.concatenate([couple[0] for couple in earlier[::-1]] + [keys], axis=0)
    value_rows = jnp.concatenate([couple[1] for couple in earlier[::-1]] + [values], axis=0)
    owner_positions = device * block_rows + jnp.arange(block_rows, dtype=jnp.int32)
    owner_starts = doc_start(lengths, owner_positions)
    key_positions = (device - SPAN) * block_rows + jnp.arange(
        (SPAN + 1) * block_rows, dtype=jnp.int32
    )
    visible = (key_positions[None, :] >= owner_starts[:, None]) & (
        key_positions[None, :] <= owner_positions[:, None]
    )
    first_row = 0 * block_rows
    attended, query_grad, key_part, value_part = attend(
        queries, key_rows, value_rows, d_attended, visible, HD
    )
    padding = jnp.zeros((first_row, key_part.shape[1]), jnp.float32)
    attended, query_grad, key_all, value_all = (
        attended,
        query_grad,
        jnp.concatenate([padding, key_part], axis=0),
        jnp.concatenate([padding, value_part], axis=0),
    )
    projected = jnp.dot(attended, group_weight, preferred_element_type=jnp.float32)
    layer_out = sent_and_summed(projected.astype(jnp.bfloat16), "head", 1).astype(jnp.bfloat16)

    def block_of(all_rows, offset):
        return all_rows[(SPAN - offset) * block_rows : (SPAN - offset + 1) * block_rows]

    key_home = block_of(key_all, 0)
    value_home = block_of(value_all, 0)
    for offset in range(1, SPAN + 1):
        returned = (
            passed_along(block_of(key_all, offset).astype(jnp.bfloat16), DP, -offset).astype(
                jnp.float32
            ),
            passed_along(block_of(value_all, offset).astype(jnp.bfloat16), DP, -offset).astype(
                jnp.float32
            ),
        )
        key_home = key_home + returned[0]
        value_home = value_home + returned[1]
    return (layer_out, query_grad, key_home.astype(jnp.bfloat16), value_home.astype(jnp.bfloat16))


def solution(mesh):
    finer = Mesh(mesh.devices.reshape(16, 4, mesh.shape["head"]), ("dp_0", "dp_1", "head"))
    placed = (P(DP, "head"), P(DP, "head"), P(DP, "head"), P(DP, "head"), P(HEAD_DP, None), P())
    return jax.shard_map(
        on_device,
        mesh=finer,
        in_specs=placed,
        out_specs=(P(DP, "head"), P(DP, "head"), P(DP, "head"), P(DP, "head")),
        check_vma=False,
    )
```

profile of v0, /device:TPU:46, one launch (start us, length us, event | category | flops | bytes accessed | tf_op | source)
XLA Modules:
  0.0 230.2 jit_solution(14787751482215236873)
XLA Ops:
  7.2 0.0 copy-start
  7.2 0.0 copy-start.2
  7.2 0.0 copy-start.5
  7.2 0.0 all-gather.2.cloned.1.call-start
  7.2 0.7 all-gather.2.cloned.1.call-update
  7.9 3.7 %collective-permute-start.3 = (bf16[256,128]{1,0:T(8,128)(2,1)}, bf16[256,128]{1,0:T(8,128)(2,1)S(1)}, u32[]{:S(2)}, u32[]{:S(2)}) collective-permute-start(bf16[256,128]{1,0:T(8,128)(2,1)} %param.7), channel_id=1, source_target_pairs={{0,8},{8,16},{16,24},{24,32},{32,40},{40,48},{48,56},{56,64},{64,7... | collective-permute-start | bytes 196616 | tf_op jit(solution)/shard_map/ppermute | solution.py:40
  11.7 4.3 %collective-permute-start.2 = (bf16[256,128]{1,0:T(8,128)(2,1)}, bf16[256,128]{1,0:T(8,128)(2,1)S(1)}, u32[]{:S(2)}, u32[]{:S(2)}) collective-permute-start(bf16[256,128]{1,0:T(8,128)(2,1)} %param.7), channel_id=1, source_target_pairs={{0,16},{8,24},{16,32},{24,40},{32,48},{40,56},{48,64},{56,72},{64,... | collective-permute-start | bytes 196616 | tf_op jit(solution)/shard_map/ppermute | solution.py:40
  16.0 0.9 copy.60
  17.0 3.7 %collective-permute-start.1 = (bf16[256,128]{0,1:T(8,128)(2,1)S(1)}, bf16[256,128]{0,1:T(8,128)(2,1)}, u32[]{:S(2)}, u32[]{:S(2)}) collective-permute-start(bf16[256,128]{0,1:T(8,128)(2,1)S(1)} %copy.60), channel_id=1, source_target_pairs={{0,8},{8,16},{16,24},{24,32},{32,40},{40,48},{48,56},{56,64},{64,7... | collective-permute-start | bytes 196616 | tf_op jit(solution)/shard_map/ppermute | solution.py:40
  20.7 3.5 %collective-permute-start = (bf16[256,128]{0,1:T(8,128)(2,1)S(1)}, bf16[256,128]{0,1:T(8,128)(2,1)}, u32[]{:S(2)}, u32[]{:S(2)}) collective-permute-start(bf16[256,128]{0,1:T(8,128)(2,1)S(1)} %copy.60), channel_id=1, source_target_pairs={{0,16},{8,24},{16,32},{24,40},{32,48},{40,56},{48,64},{56,72},{64,... | collective-permute-start | bytes 196616 | tf_op jit(solution)/shard_map/ppermute | solution.py:40
  24.1 1.1 copy.67
  25.2 1.4 broadcast_in_dim.30
  26.7 4.9 %all-to-all-start.1 = ((bf16[8,256,512]{1,2,0:T(8,128)(2,1)}), bf16[8,256,512]{1,2,0:T(8,128)(2,1)S(1)}, u32[]{:S(2)}, u32[]{:S(2)}) async-start(bf16[8,256,512]{1,2,0:T(8,128)(2,1)} %broadcast_in_dim.30), calls=%async_computation.1 | async-start | bytes 4194304 | tf_op jit(solution)/shard_map/all_to_all | solution.py:30
  31.6 0.0 copy-done.5
  31.6 0.1 copy.63
  31.7 0.1 reduce-window.8
  31.8 0.1 reduce.4
  31.9 0.1 select_reduce_fusion
  32.0 0.2 compare_and_fusion
  32.3 0.0 collective-permute-done.3
  32.3 0.0 collective-permute-done.2
  32.3 0.0 copy-done
  32.3 0.0 copy-done.2
  32.3 0.0 copy-start.3
  32.3 1.1 fusion.5
  33.4 0.0 copy-start.1
  33.5 1.3 fusion.4
  34.8 0.0 copy-done.3
  34.8 1.4 copy-done.1
  36.1 3.1 %convert_bitcast_fusion = bf16[8,256,768]{1,2,0:T(8,128)(2,1)} fusion(f32[8,256]{1,0:T(8,128)S(1)} %fusion.4, f32[8,256]{1,0:T(8,128)S(1)} %get-tuple-element.24, f32[768,256,8]{1,0,2:T(8,128)S(1)} %get-tuple-element.25, pred[256,768]{0,1:T(8,128)(4,1)S(1)} %compare_and_fusion), kind=kLoop, calls=%fused_computation.11 | loop fusion | flops 7864320 | bytes 9650176 | tf_op jit(solution)/shard_map/reshape.20
  39.2 5.1 %copy.74 = bf16[8,256,768]{2,0,1:T(8,128)(2,1)} copy(bf16[8,256,768]{1,2,0:T(8,128)(2,1)} %convert_bitcast_fusion) | data formatting | bytes 6291456 | tf_op jit(solution)/shard_map/reshape.20
  44.3 13.0 %all-to-all-done.1 = bf16[8,256,512]{1,2,0:T(8,128)(2,1)S(1)} async-done(((bf16[8,256,512]{1,2,0:T(8,128)(2,1)}), bf16[8,256,512]{1,2,0:T(8,128)(2,1)S(1)}, u32[]{:S(2)}, u32[]{:S(2)}) %all-to-all-start.1) | async-done | bytes 2097184 | tf_op jit(solution)/shard_map/all_to_all | solution.py:30
  57.3 111.5 %all-gather.2.cloned.1.call-done = bf16[1024,4096]{1,0:T(8,128)(2,1)} async-done(((bf16[16,4096]{1,0:T(8,128)(2,1)}), bf16[1024,4096]{1,0:T(8,128)(2,1)}) %all-gather.2.cloned.1.call-update) | async-done | bytes 8388624 | tf_op jit(solution)/shard_map/all_gather | solution.py:103
  168.9 5.8 %convolution_convert_fusion.1 = bf16[256,1024]{1,0:T(8,128)(2,1)S(1)} fusion(bf16[256,4096]{0,1:T(8,128)(2,1)S(1)} %bitcast.148, bf16[1024,4096]{1,0:T(8,128)(2,1)} %all-gather.2.cloned.1.call-done), kind=kOutput, calls=%fused_computation.13 | convolution fusion | flops 2147745792 | bytes 11010048 | tf_op jit(solution)/shard_map/tc,rc->tr/dot_general | solution.py:105
  174.6 0.2 copy.70
  174.8 0.0 collective-permute-done.1
  174.8 0.0 collective-permute-done
  174.9 3.2 %multiply_reduce_fusion = (f32[256,8]{0,1:T(8,128)}, bf16[128,8,256]{2,0,1:T(8,128)(2,1)S(1)}) fusion(f32[256,1,8,128]{0,3,2,1:T(8,128)S(1)} %bitcast.145, bf16[8,256,768]{1,2,0:T(8,128)(2,1)} %convert_bitcast_fusion, bf16[256,128]{0,1:T(8,128)(2,1)S(1)} %copy.60, bf16[256,128]{0,1:T(8,128)(2,1)} %collective-permute-done.1, ...), kind=kOutput, calls=%fused_computation.18 | convolution fusion | flops 404289536 | bytes 4923392 | tf_op jit(solution)/shard_map/grtn,ngd->tgrd/dot_general | solution.py:77
  178.0 5.8 %convolution_convert_fusion = bf16[256,4096]{1,0:T(8,128)(2,1)S(1)} fusion(bf16[256,1024]{0,1:T(8,128)(2,1)S(1)} %bitcast.146, bf16[1024,4096]{1,0:T(8,128)(2,1)} %all-gather.2.cloned.1.call-done), kind=kOutput, calls=%fused_computation.8 | convolution fusion | flops 2148532224 | bytes 11010048 | tf_op jit(solution)/shard_map/dot_general | solution.py:130
  183.8 1.6 copy.104
  185.3 5.0 %all-to-all-start = ((bf16[8,256,512]{2,1,0:T(8,128)(2,1)}), bf16[8,256,512]{2,1,0:T(8,128)(2,1)S(1)}, u32[]{:S(2)}, u32[]{:S(2)}) async-start(bf16[8,256,512]{2,1,0:T(8,128)(2,1)} %bitcast.144), calls=%async_computation | async-start | bytes 4194304 | tf_op jit(solution)/shard_map/all_to_all | solution.py:50
  190.4 0.1 copy.86
  190.5 3.3 %fusion.25 = (bf16[768,1,128]{0,2,1:T(8,128)(2,1)S(1)}, f32[768,1,128]{0,2,1:T(8,128)}) fusion(bf16[256,8,128]{2,1,0:T(8,128)(2,1)S(1)} %bitcast.150, bf16[8,256,768]{2,0,1:T(8,128)(2,1)} %copy.74), kind=kOutput, calls=%fused_computation.49 | convolution fusion | flops 402751488 | bytes 4259840 | tf_op jit(solution)/shard_map/grtn,tgrd->ngd/dot_general | solution.py:89
  193.8 0.7 slice_bitcast_fusion.3
  194.4 3.7 %collective-permute-start.7 = (bf16[256,128]{0,1:T(8,128)(2,1)}, bf16[256,128]{0,1:T(8,128)(2,1)}, u32[]{:S(2)}, u32[]{:S(2)}) collective-permute-start(bf16[256,128]{0,1:T(8,128)(2,1)} %get-tuple-element.21), channel_id=1, source_target_pairs={{16,0},{24,8},{32,16},{40,24},{48,32},{56,40},{64,48},{72,56},{80,... | collective-permute-start | bytes 196616 | tf_op jit(solution)/shard_map/ppermute | solution.py:40
  198.2 3.3 %collective-permute-start.6 = (bf16[256,128]{0,1:T(8,128)(2,1)}, bf16[256,128]{0,1:T(8,128)(2,1)}, u32[]{:S(2)}, u32[]{:S(2)}) collective-permute-start(bf16[256,128]{0,1:T(8,128)(2,1)} %get-tuple-element.20), channel_id=1, source_target_pairs={{8,0},{16,8},{24,16},{32,24},{40,32},{48,40},{56,48},{64,56},{72,6... | collective-permute-start | bytes 196616 | tf_op jit(solution)/shard_map/ppermute | solution.py:40
  201.5 0.0 copy-start.4
  201.5 4.5 %fusion.6 = bf16[8,256,768]{1,2,0:T(8,128)(2,1)S(1)} fusion(f32[8,256]{1,0:T(8,128)} %bitcast.151, f32[8,256]{1,0:T(8,128)S(1)} %fusion.4, f32[8,256]{1,0:T(8,128)S(1)} %get-tuple-element.24, f32[768,256,8]{1,0,2:T(8,128)} %copy-done.1, pred[256,768]{0,1:T(8,128)(4,1)S(1)} %compare_and_fusion, bf16[256,128]{0,1:T(8,128)(2,1)S(1)} %copy.60, ...), kind=kOutput, calls=%fused_computation.10 | convolution fusion | flops 415825920 | bytes 10379264 | tf_op jit(solution)/shard_map/tgrd,ngd->grtn/dot_general | solution.py:81
  206.0 0.0 copy-done.4
  206.0 0.6 convolution_convert_fusion.2
  206.6 1.0 fusion.24
  207.6 0.7 slice_bitcast_fusion.5
  208.3 1.0 copy.75
  209.3 3.9 %collective-permute-start.5 = (bf16[256,128]{1,0:T(8,128)(2,1)}, bf16[256,128]{1,0:T(8,128)(2,1)S(1)}, u32[]{:S(2)}, u32[]{:S(2)}) collective-permute-start(bf16[256,128]{1,0:T(8,128)(2,1)} %get-tuple-element.23), channel_id=1, source_target_pairs={{16,0},{24,8},{32,16},{40,24},{48,32},{56,40},{64,48},{72,56},{80,... | collective-permute-start | bytes 196616 | tf_op jit(solution)/shard_map/ppermute | solution.py:40
  213.2 2.7 %collective-permute-start.4 = (bf16[256,128]{1,0:T(8,128)(2,1)}, bf16[256,128]{1,0:T(8,128)(2,1)S(1)}, u32[]{:S(2)}, u32[]{:S(2)}) collective-permute-start(bf16[256,128]{1,0:T(8,128)(2,1)} %get-tuple-element.22), channel_id=1, source_target_pairs={{8,0},{16,8},{24,16},{32,24},{40,32},{48,40},{56,48},{64,56},{72,6... | collective-permute-start | bytes 196616 | tf_op jit(solution)/shard_map/ppermute | solution.py:40
  215.9 0.0 collective-permute-done.7
  215.9 0.0 collective-permute-done.6
  216.0 1.0 fusion.16
  216.9 0.7 copy.76
  217.7 0.4 collective-permute-done.5
  218.1 3.6 %collective-permute-done.4 = bf16[256,128]{1,0:T(8,128)(2,1)S(1)} collective-permute-done((bf16[256,128]{1,0:T(8,128)(2,1)}, bf16[256,128]{1,0:T(8,128)(2,1)S(1)}, u32[]{:S(2)}, u32[]{:S(2)}) %collective-permute-start.4) | collective-permute-done | bytes 65568 | tf_op jit(solution)/shard_map/ppermute | solution.py:40
  221.7 0.7 fusion.19
  222.3 0.0 all-to-all-done
  222.3 1.0 reduce_sum.43
  (2 shorter events, 0.0 us)
Async XLA Ops:
  7.2 25.1 %copy-start = (bf16[256,1024]{1,0:T(8,128)(2,1)S(1)}, bf16[256,1024]{1,0:T(8,128)(2,1)}, u32[]{:S(2)}) copy-start(bf16[256,1024]{1,0:T(8,128)(2,1)} %param.6) | copy-start | bytes 1572868
  7.2 25.1 %copy-start.2 = (bf16[256,128]{1,0:T(8,128)(2,1)S(1)}, bf16[256,128]{1,0:T(8,128)(2,1)}, u32[]{:S(2)}) copy-start(bf16[256,128]{1,0:T(8,128)(2,1)} %param.7) | copy-start | bytes 196612
  7.2 24.4 %copy-start.5 = (s32[64]{0:T(128)S(1)}, s32[64]{0:T(128)}, u32[]{:S(2)}) copy-start(s32[64]{0:T(128)} %param.11) | copy-start | bytes 772
  7.2 161.7 %all-gather.2.cloned.1.call-start = ((), (), s32[]{:S(2)}) async-start(), calls=%async_computation.2 | async-start | bytes 8519680 | tf_op jit(solution)/shard_map/all_gather | solution.py:103
  7.9 24.3 %collective-permute-start.3 = (bf16[256,128]{1,0:T(8,128)(2,1)}, bf16[256,128]{1,0:T(8,128)(2,1)S(1)}, u32[]{:S(2)}, u32[]{:S(2)}) collective-permute-start(bf16[256,128]{1,0:T(8,128)(2,1)} %param.7), channel_id=1, source_target_pairs={{0,8},{8,16},{16,24},{24,32},{32,40},{40,48},{48,56},{56,64},{64,7... | collective-permute-start | bytes 196616 | tf_op jit(solution)/shard_map/ppermute | solution.py:40
  11.7 20.6 %collective-permute-start.2 = (bf16[256,128]{1,0:T(8,128)(2,1)}, bf16[256,128]{1,0:T(8,128)(2,1)S(1)}, u32[]{:S(2)}, u32[]{:S(2)}) collective-permute-start(bf16[256,128]{1,0:T(8,128)(2,1)} %param.7), channel_id=1, source_target_pairs={{0,16},{8,24},{16,32},{24,40},{32,48},{40,56},{48,64},{56,72},{64,... | collective-permute-start | bytes 196616 | tf_op jit(solution)/shard_map/ppermute | solution.py:40
  17.0 157.9 %collective-permute-start.1 = (bf16[256,128]{0,1:T(8,128)(2,1)S(1)}, bf16[256,128]{0,1:T(8,128)(2,1)}, u32[]{:S(2)}, u32[]{:S(2)}) collective-permute-start(bf16[256,128]{0,1:T(8,128)(2,1)S(1)} %copy.60), channel_id=1, source_target_pairs={{0,8},{8,16},{16,24},{24,32},{32,40},{40,48},{48,56},{56,64},{64,7... | collective-permute-start | bytes 196616 | tf_op jit(solution)/shard_map/ppermute | solution.py:40
  20.7 154.2 %collective-permute-start = (bf16[256,128]{0,1:T(8,128)(2,1)S(1)}, bf16[256,128]{0,1:T(8,128)(2,1)}, u32[]{:S(2)}, u32[]{:S(2)}) collective-permute-start(bf16[256,128]{0,1:T(8,128)(2,1)S(1)} %copy.60), channel_id=1, source_target_pairs={{0,16},{8,24},{16,32},{24,40},{32,48},{40,56},{48,64},{56,72},{64,... | collective-permute-start | bytes 196616 | tf_op jit(solution)/shard_map/ppermute | solution.py:40
  26.7 30.6 %all-to-all-start.1 = ((bf16[8,256,512]{1,2,0:T(8,128)(2,1)}), bf16[8,256,512]{1,2,0:T(8,128)(2,1)S(1)}, u32[]{:S(2)}, u32[]{:S(2)}) async-start(bf16[8,256,512]{1,2,0:T(8,128)(2,1)} %broadcast_in_dim.30), calls=%async_computation.1 | async-start | bytes 4194304 | tf_op jit(solution)/shard_map/all_to_all | solution.py:30
  32.3 2.5 %copy-start.3 = (bf16[256,128]{1,0:T(8,128)(2,1)}, bf16[256,128]{1,0:T(8,128)(2,1)S(1)}, u32[]{:S(2)}) copy-start(bf16[256,128]{1,0:T(8,128)(2,1)S(1)} %collective-permute-done.2) | copy-start | bytes 196612
  33.4 2.7 %copy-start.1 = (f32[768,256,8]{1,0,2:T(8,128)}, f32[768,256,8]{1,0,2:T(8,128)S(1)}, u32[]{:S(2)}) copy-start(f32[768,256,8]{1,0,2:T(8,128)S(1)} %get-tuple-element.25) | copy-start | bytes 18874372
  185.3 37.0 %all-to-all-start = ((bf16[8,256,512]{2,1,0:T(8,128)(2,1)}), bf16[8,256,512]{2,1,0:T(8,128)(2,1)S(1)}, u32[]{:S(2)}, u32[]{:S(2)}) async-start(bf16[8,256,512]{2,1,0:T(8,128)(2,1)} %bitcast.144), calls=%async_computation | async-start | bytes 4194304 | tf_op jit(solution)/shard_map/all_to_all | solution.py:50
  194.4 21.5 %collective-permute-start.7 = (bf16[256,128]{0,1:T(8,128)(2,1)}, bf16[256,128]{0,1:T(8,128)(2,1)}, u32[]{:S(2)}, u32[]{:S(2)}) collective-permute-start(bf16[256,128]{0,1:T(8,128)(2,1)} %get-tuple-element.21), channel_id=1, source_target_pairs={{16,0},{24,8},{32,16},{40,24},{48,32},{56,40},{64,48},{72,56},{80,... | collective-permute-start | bytes 196616 | tf_op jit(solution)/shard_map/ppermute | solution.py:40
  198.2 17.8 %collective-permute-start.6 = (bf16[256,128]{0,1:T(8,128)(2,1)}, bf16[256,128]{0,1:T(8,128)(2,1)}, u32[]{:S(2)}, u32[]{:S(2)}) collective-permute-start(bf16[256,128]{0,1:T(8,128)(2,1)} %get-tuple-element.20), channel_id=1, source_target_pairs={{8,0},{16,8},{24,16},{32,24},{40,32},{48,40},{56,48},{64,56},{72,6... | collective-permute-start | bytes 196616 | tf_op jit(solution)/shard_map/ppermute | solution.py:40
  201.5 4.5 %copy-start.4 = (bf16[256,128]{1,0:T(8,128)(2,1)S(1)}, bf16[256,128]{1,0:T(8,128)(2,1)}, u32[]{:S(2)}) copy-start(bf16[256,128]{1,0:T(8,128)(2,1)} %copy-done.3) | copy-start | bytes 196612
  209.3 8.8 %collective-permute-start.5 = (bf16[256,128]{1,0:T(8,128)(2,1)}, bf16[256,128]{1,0:T(8,128)(2,1)S(1)}, u32[]{:S(2)}, u32[]{:S(2)}) collective-permute-start(bf16[256,128]{1,0:T(8,128)(2,1)} %get-tuple-element.23), channel_id=1, source_target_pairs={{16,0},{24,8},{32,16},{40,24},{48,32},{56,40},{64,48},{72,56},{80,... | collective-permute-start | bytes 196616 | tf_op jit(solution)/shard_map/ppermute | solution.py:40
  213.2 8.5 %collective-permute-start.4 = (bf16[256,128]{1,0:T(8,128)(2,1)}, bf16[256,128]{1,0:T(8,128)(2,1)S(1)}, u32[]{:S(2)}, u32[]{:S(2)}) collective-permute-start(bf16[256,128]{1,0:T(8,128)(2,1)} %get-tuple-element.22), channel_id=1, source_target_pairs={{8,0},{16,8},{24,16},{32,24},{40,32},{48,40},{56,48},{64,56},{72,6... | collective-permute-start | bytes 196616 | tf_op jit(solution)/shard_map/ppermute | solution.py:40
Sparse Core Ops, SparseCore 0:
  11.0 157.8 all-gather.1
where the time goes:
time: 231 us; the launch traced here: 230 us
  waiting for transfers between devices  129 us (56%)
  starting transfers between devices  38.9 us (17%)
  matrix products  25.2 us (11%)
  local copies, waits for them, and re-layouts  15 us (6%)
  between operations  14.3 us (6%)
  other arithmetic  7.6 us (3%)
    all_gather x1, waiting for transfers between devices, on_device(): group_weight = lax.all_gather(out_weight, DP, axis=0, tiled=True)  112 us
    ppermute x8, starting transfers between devices, passed_along(): return lax.ppermute(block, axis, route)  28.9 us
    all_to_all x1, waiting for transfers between devices, from_everyone(): lax.all_to_all(jnp.broadcast_to(x[None], (size, *x.shape)), axis, 0, 0, t...  13 us
    dot_general x1, matrix products, on_device(): jnp.einsum('tc,rc->tr', upstream_all, group_weight, preferred_element_typ...  5.76 us
    dot_general x1, matrix products, on_device(): jnp.dot(attended, group_weight, preferred_element_type=jnp.float32)  5.75 us
    unnamed x17, local copies, waits for them, and re-layouts  5.25 us
    another operation x2, local copies, waits for them, and re-layouts  5.16 us
    all_to_all x1, starting transfers between devices, sent_and_summed(): lax.all_to_all(pieces, axis, split_axis=0, concat_axis=0, tiled=True)  5.02 us
  transfers between devices with their start and end apart: 11, of which 4 were waited for; matrix products, arithmetic and copies ran while one was open for 15% of the time, Pallas kernels for 0%

commit v1 on v0

--- a/solution.py
+++ b/solution.py
@@ -100,7 +100,9 @@
 def on_device(queries, keys, values, output_grad, out_weight, lengths):
     block_rows = queries.shape[0]
     device = lax.axis_index(DP)
-    group_weight = lax.all_gather(out_weight, DP, axis=0, tiled=True)
+    group_weight = jnp.concatenate(
+        lax.all_to_all(jnp.stack([out_weight] * lax.axis_size(DP)), DP, 0, 0), axis=0
+    )
     upstream_all = gather_directly(output_grad, "head", 1)
     d_attended = jnp.einsum(
         "tc,rc->tr", upstream_all, group_weight, preferred_element_type=jnp.float32

time: 231 us -> 484 us (2.10)
  the two profiles are of different devices: /device:TPU:46 before, /device:TPU:110 now
where the time goes in v1:
time: 484 us
  waiting for transfers between devices  349 us (72%)
  starting transfers between devices  53.3 us (11%)
  blocking collectives  30.7 us (6%)
  matrix products  25.1 us (5%)
  local copies, waits for them, and re-layouts  17.1 us (4%)
  other arithmetic  7.62 us (2%)
    ppermute x8, waiting for transfers between devices, passed_along(): return lax.ppermute(block, axis, route)  349 us
    ppermute x8, starting transfers between devices, passed_along(): return lax.ppermute(block, axis, route)  31 us
    all_to_all x1, blocking collectives, from_everyone(): lax.all_to_all(jnp.broadcast_to(x[None], (size, *x.shape)), axis, 0, 0, t...  30.7 us
    all_to_all x1, starting transfers between devices, on_device(): lax.all_to_all(jnp.stack([out_weight] * lax.axis_size(DP)), DP, 0, 0)  17.5 us
  transfers between devices with their start and end apart: 10, of which 4 were waited for; matrix products, arithmetic and copies ran while one was open for 6% of the time, Pallas kernels for 0%

profile of v1, /device:TPU:110, one launch (start us, length us, event | category | flops | bytes accessed | tf_op | source)
XLA Modules:
  0.0 483.7 jit_solution(2114426781003863295)
XLA Ops:
  0.6 0.0 copy-start
  0.6 0.0 copy-start.2
  0.7 1.2 copy.67
  1.8 0.1 broadcast_in_dim.30
  2.0 30.7 %all_to_all.15 = bf16[8,256,512]{1,2,0:T(8,128)(2,1)S(1)} all-to-all(bf16[8,256,512]{1,2,0:T(8,128)(2,1)S(1)} %broadcast_in_dim.30), channel_id=1, replica_groups=mesh['dp_0'=16,'dp_1'=4,'head'=8] {'head'}, dimensions={0} | all-to-all | bytes 4194304 | tf_op jit(solution)/shard_map/all_to_all | solution.py:30
  32.7 0.0 copy-done.2
  32.7 4.3 stack.2
  36.9 0.0 copy-start.3
  36.9 17.5 %all-to-all-start = ((bf16[64,16,4096]{2,1,0:T(8,128)(2,1)}), bf16[64,16,4096]{2,1,0:T(8,128)(2,1)}, u32[]{:S(2)}, u32[]{:S(2)}) async-start(bf16[64,16,4096]{2,1,0:T(8,128)(2,1)} %stack.2), calls=%async_computation | async-start | bytes 16777216 | tf_op jit(solution)/shard_map/all_to_all | solution.py:104
  54.5 0.0 copy-done.3
  54.5 4.6 collective-permute-start.3
  59.1 4.3 collective-permute-start.2
  63.4 0.0 copy-done.6
  63.4 0.1 copy.60
  63.5 3.7 collective-permute-start.1
  67.2 3.3 collective-permute-start
  70.4 0.0 copy-done.7
  70.5 0.1 copy.63
  70.6 0.1 reduce-window.8
  70.7 0.1 reduce.4
  70.8 0.1 select_reduce_fusion
  70.9 0.2 compare_and_fusion
  71.1 341.7 %collective-permute-done.3 = bf16[256,128]{1,0:T(8,128)(2,1)S(1)} collective-permute-done((bf16[256,128]{1,0:T(8,128)(2,1)S(1)}, bf16[256,128]{1,0:T(8,128)(2,1)S(1)}, u32[]{:S(2)}, u32[]{:S(2)}) %collective-permute-start.3) | collective-permute-done | bytes 65568 | tf_op jit(solution)/shard_map/ppermute | solution.py:40
  412.9 2.5 collective-permute-done.2
  415.4 0.0 copy-done
  415.4 1.1 fusion.5
  416.5 0.0 copy-start.1
  416.5 1.3 fusion.4
  417.8 0.0 copy-done.4
  417.8 1.3 copy-done.1
  419.1 3.1 convert_bitcast_fusion
  422.3 5.1 %copy.74 = bf16[8,256,768]{2,0,1:T(8,128)(2,1)} copy(bf16[8,256,768]{1,2,0:T(8,128)(2,1)} %convert_bitcast_fusion) | data formatting | bytes 6291456 | tf_op jit(solution)/shard_map/reshape.10
  427.3 0.0 all-to-all-done
  427.3 5.8 %convolution_convert_fusion.1 = bf16[256,1024]{1,0:T(8,128)(2,1)S(1)} fusion(bf16[256,4096]{0,1:T(8,128)(2,1)S(1)} %bitcast.149, bf16[1024,4096]{1,0:T(8,128)(2,1)} %bitcast.9), kind=kOutput, calls=%fused_computation.13 | convolution fusion | flops 2147745792 | bytes 11010048 | tf_op jit(solution)/shard_map/tc,rc->tr/dot_general | solution.py:107
  433.1 0.2 copy.70
  433.3 0.0 collective-permute-done.1
  433.3 0.0 collective-permute-done
  433.3 3.2 multiply_reduce_fusion
  436.5 5.8 %convolution_convert_fusion = bf16[256,4096]{1,0:T(8,128)(2,1)S(1)} fusion(bf16[256,1024]{0,1:T(8,128)(2,1)S(1)} %bitcast.147, bf16[1024,4096]{1,0:T(8,128)(2,1)} %bitcast.9), kind=kOutput, calls=%fused_computation.8 | convolution fusion | flops 2148532224 | bytes 11010048 | tf_op jit(solution)/shard_map/dot_general | solution.py:132
  442.2 1.5 copy.104
  443.8 4.7 all-to-all-start.1
  448.5 0.1 copy.86
  448.6 3.3 fusion.25
  451.9 0.7 slice_bitcast_fusion.3
  452.6 7.7 %collective-permute-start.7 = (bf16[256,128]{0,1:T(8,128)(2,1)}, bf16[256,128]{0,1:T(8,128)(2,1)}, u32[]{:S(2)}, u32[]{:S(2)}) collective-permute-start(bf16[256,128]{0,1:T(8,128)(2,1)} %get-tuple-element.21), channel_id=1, source_target_pairs={{16,0},{24,8},{32,16},{40,24},{48,32},{56,40},{64,48},{72,56},{80,... | collective-permute-start | bytes 196616 | tf_op jit(solution)/shard_map/ppermute | solution.py:40
  460.3 2.1 collective-permute-start.6
  462.4 0.0 copy-start.5
  462.4 4.5 fusion.6
  466.9 0.0 copy-done.5
  466.9 0.6 convolution_convert_fusion.2
  467.5 1.0 fusion.24
  468.5 0.7 slice_bitcast_fusion.5
  469.2 1.0 copy.75
  470.2 2.1 collective-permute-start.5
  472.3 3.2 collective-permute-start.4
  475.5 0.0 collective-permute-done.7
  475.6 0.0 collective-permute-done.6
  475.6 1.0 fusion.16
  476.5 0.7 copy.76
  477.3 3.1 collective-permute-done.5
  480.4 1.7 collective-permute-done.4
  482.0 0.7 fusion.19
  482.7 0.0 all-to-all-done.1
  482.7 1.0 reduce_sum.43
  (5 shorter events, 0.0 us)
Async XLA Ops:
  0.6 414.8 %copy-start = (bf16[256,1024]{1,0:T(8,128)(2,1)S(1)}, bf16[256,1024]{1,0:T(8,128)(2,1)}, u32[]{:S(2)}) copy-start(bf16[256,1024]{1,0:T(8,128)(2,1)} %param.6) | copy-start | bytes 1572868
  0.6 32.0 %copy-start.2 = (bf16[16,4096]{1,0:T(8,128)(2,1)S(1)}, bf16[16,4096]{1,0:T(8,128)(2,1)}, u32[]{:S(2)}) copy-start(bf16[16,4096]{1,0:T(8,128)(2,1)} %param.10) | copy-start | bytes 393220
  36.9 17.6 %copy-start.3 = (bf16[256,128]{1,0:T(8,128)(2,1)S(1)}, bf16[256,128]{1,0:T(8,128)(2,1)}, u32[]{:S(2)}) copy-start(bf16[256,128]{1,0:T(8,128)(2,1)} %param.7) | copy-start | bytes 196612
  36.9 26.4 %copy-start.6 = (bf16[256,128]{1,0:T(8,128)(2,1)S(1)}, bf16[256,128]{1,0:T(8,128)(2,1)}, u32[]{:S(2)}) copy-start(bf16[256,128]{1,0:T(8,128)(2,1)} %param.8) | copy-start | bytes 196612
  36.9 33.5 %copy-start.7 = (s32[64]{0:T(128)S(1)}, s32[64]{0:T(128)}, u32[]{:S(2)}) copy-start(s32[64]{0:T(128)} %param.11) | copy-start | bytes 772
  36.9 390.4 %all-to-all-start = ((bf16[64,16,4096]{2,1,0:T(8,128)(2,1)}), bf16[64,16,4096]{2,1,0:T(8,128)(2,1)}, u32[]{:S(2)}, u32[]{:S(2)}) async-start(bf16[64,16,4096]{2,1,0:T(8,128)(2,1)} %stack.2), calls=%async_computation | async-start | bytes 16777216 | tf_op jit(solution)/shard_map/all_to_all | solution.py:104
  54.5 358.4 %collective-permute-start.3 = (bf16[256,128]{1,0:T(8,128)(2,1)S(1)}, bf16[256,128]{1,0:T(8,128)(2,1)S(1)}, u32[]{:S(2)}, u32[]{:S(2)}) collective-permute-start(bf16[256,128]{1,0:T(8,128)(2,1)S(1)} %copy-done.3), channel_id=1, source_target_pairs={{0,8},{8,16},{16,24},{24,32},{32,40},{40,48},{48,56},{56,64},{64,7... | collective-permute-start | bytes 196616 | tf_op jit(solution)/shard_map/ppermute | solution.py:40
  59.1 356.3 %collective-permute-start.2 = (bf16[256,128]{1,0:T(8,128)(2,1)S(1)}, bf16[256,128]{1,0:T(8,128)(2,1)S(1)}, u32[]{:S(2)}, u32[]{:S(2)}) collective-permute-start(bf16[256,128]{1,0:T(8,128)(2,1)S(1)} %copy-done.3), channel_id=1, source_target_pairs={{0,16},{8,24},{16,32},{24,40},{32,48},{40,56},{48,64},{56,72},{64,... | collective-permute-start | bytes 196616 | tf_op jit(solution)/shard_map/ppermute | solution.py:40
  63.5 369.8 %collective-permute-start.1 = (bf16[256,128]{0,1:T(8,128)(2,1)S(1)}, bf16[256,128]{0,1:T(8,128)(2,1)}, u32[]{:S(2)}, u32[]{:S(2)}) collective-permute-start(bf16[256,128]{0,1:T(8,128)(2,1)S(1)} %copy.60), channel_id=1, source_target_pairs={{0,8},{8,16},{16,24},{24,32},{32,40},{40,48},{48,56},{56,64},{64,7... | collective-permute-start | bytes 196616 | tf_op jit(solution)/shard_map/ppermute | solution.py:40
  67.2 366.1 %collective-permute-start = (bf16[256,128]{0,1:T(8,128)(2,1)S(1)}, bf16[256,128]{0,1:T(8,128)(2,1)}, u32[]{:S(2)}, u32[]{:S(2)}) collective-permute-start(bf16[256,128]{0,1:T(8,128)(2,1)S(1)} %copy.60), channel_id=1, source_target_pairs={{0,16},{8,24},{16,32},{24,40},{32,48},{40,56},{48,64},{56,72},{64,... | collective-permute-start | bytes 196616 | tf_op jit(solution)/shard_map/ppermute | solution.py:40
  415.4 2.4 copy-start.4
  416.5 2.6 copy-start.1
  443.8 38.9 %all-to-all-start.1 = ((bf16[8,256,512]{2,1,0:T(8,128)(2,1)}), bf16[8,256,512]{2,1,0:T(8,128)(2,1)S(1)}, u32[]{:S(2)}, u32[]{:S(2)}) async-start(bf16[8,256,512]{2,1,0:T(8,128)(2,1)} %bitcast.145), calls=%async_computation.1 | async-start | bytes 4194304 | tf_op jit(solution)/shard_map/all_to_all | solution.py:50
  452.6 23.0 %collective-permute-start.7 = (bf16[256,128]{0,1:T(8,128)(2,1)}, bf16[256,128]{0,1:T(8,128)(2,1)}, u32[]{:S(2)}, u32[]{:S(2)}) collective-permute-start(bf16[256,128]{0,1:T(8,128)(2,1)} %get-tuple-element.21), channel_id=1, source_target_pairs={{16,0},{24,8},{32,16},{40,24},{48,32},{56,40},{64,48},{72,56},{80,... | collective-permute-start | bytes 196616 | tf_op jit(solution)/shard_map/ppermute | solution.py:40
  460.3 15.3 %collective-permute-start.6 = (bf16[256,128]{0,1:T(8,128)(2,1)}, bf16[256,128]{0,1:T(8,128)(2,1)}, u32[]{:S(2)}, u32[]{:S(2)}) collective-permute-start(bf16[256,128]{0,1:T(8,128)(2,1)} %get-tuple-element.20), channel_id=1, source_target_pairs={{8,0},{16,8},{24,16},{32,24},{40,32},{48,40},{56,48},{64,56},{72,6... | collective-permute-start | bytes 196616 | tf_op jit(solution)/shard_map/ppermute | solution.py:40
  462.4 4.5 copy-start.5
  470.2 10.2 %collective-permute-start.5 = (bf16[256,128]{1,0:T(8,128)(2,1)}, bf16[256,128]{1,0:T(8,128)(2,1)S(1)}, u32[]{:S(2)}, u32[]{:S(2)}) collective-permute-start(bf16[256,128]{1,0:T(8,128)(2,1)} %get-tuple-element.23), channel_id=1, source_target_pairs={{16,0},{24,8},{32,16},{40,24},{48,32},{56,40},{64,48},{72,56},{80,... | collective-permute-start | bytes 196616 | tf_op jit(solution)/shard_map/ppermute | solution.py:40
  472.3 9.7 %collective-permute-start.4 = (bf16[256,128]{1,0:T(8,128)(2,1)}, bf16[256,128]{1,0:T(8,128)(2,1)S(1)}, u32[]{:S(2)}, u32[]{:S(2)}) collective-permute-start(bf16[256,128]{1,0:T(8,128)(2,1)} %get-tuple-element.22), channel_id=1, source_target_pairs={{8,0},{16,8},{24,16},{32,24},{40,32},{48,40},{56,48},{64,56},{72,6... | collective-permute-start | bytes 196616 | tf_op jit(solution)/shard_map/ppermute | solution.py:40
